TPU v7x, 32 devices: a whole 2x2x4 slice. The times are simulated.
32 devices in a mesh: gx: 8 (over z, y), gy: 4 (over x, core).
Axes of the slice: x: 2, y: 2, z: 4, core: 2. Of those that a mesh axis runs over, the one named last changes fastest.
Arguments:
- residual_block: float32 [8, 32, 32, 256], P(None, 'gx', 'gy'), may hold values from -70 to 70
- diagonal: float32 [32, 32, 256], P('gx', 'gy'), may hold values from 0.5 to 4
Outputs:
- correction: float32 [8, 32, 32, 256], P(None, 'gx', 'gy')
- new_residual: float32 [8, 32, 32, 256], P(None, 'gx', 'gy')
- estimate: float32 [8], replicated
All inputs are finite; a program needn't handle non-finite values.
Results may differ from a plain program's by a relative error of at most 0.008.
Values sent between devices are 32-bit elements; how exact they have to be, the bound alone decides.
A program may use at most 64 MiB of HBM per device.

v0:
```python
import jax
import jax.numpy as jnp
import numpy as np
from jax import lax
from jax.sharding import PartitionSpec as P

NRHS = 8


WEIGHT_X = 0.4
WEIGHT_Y = 0.2
WEIGHT_Z = 0.1
CENTRE = 2.2
SCALE_POWER = 3.0
SHIFTS = (6.0, 1.5, 4.5, 3.0)
EPSILON = 1e-06


def padded_2(block, sides, width):
    for axis, dim in sides:
        count = lax.axis_size(axis)
        forward = [(i, i + 1) for i in range(count - 1)]
        backward = [(target, source) for source, target in forward]
        low = lax.ppermute(
            lax.slice_in_dim(block, block.shape[dim] - width, None, axis=dim), axis, forward
        )
        high = lax.ppermute(lax.slice_in_dim(block, 0, width, axis=dim), axis, backward)
        block = jnp.concatenate([low, block, high], axis=dim)
    return block


def apply_padded(padded, diag_inner, shift_now):
    along_z = jnp.pad(padded, ((0, 0), (0, 0), (0, 0), (1, 1)))
    sum_z = padded + WEIGHT_Z * (along_z[..., :-2] + along_z[..., 2:])
    sum_y = sum_z[:, :, 1:-1] + WEIGHT_Y * (sum_z[:, :, :-2] + sum_z[:, :, 2:])
    sum_x = sum_y[:, 1:-1] + WEIGHT_X * (sum_y[:, :-2] + sum_y[:, 2:])
    centre_cells = padded[:, 1:-1, 1:-1]
    return ((CENTRE + 1.0 + diag_inner - shift_now) * centre_cells - sum_x) / SCALE_POWER


def newton_table():
    blocks = len(SHIFTS)
    identity = np.eye(NRHS, dtype=np.float32)
    matrix = np.zeros(((blocks + 1) * NRHS, blocks * NRHS), np.float32)
    for block_index in range(blocks):
        low = block_index * NRHS
        matrix[low : low + NRHS, low : low + NRHS] = SHIFTS[block_index] * identity
        matrix[low + NRHS : low + 2 * NRHS, low : low + NRHS] = SCALE_POWER * identity
    return matrix


def solve_small(gram_full):
    highest = lax.Precision.HIGHEST
    newton = jnp.asarray(newton_table(), gram_full.dtype)
    image = jnp.dot(newton.T, jnp.dot(gram_full, newton, precision=highest), precision=highest)
    right_side = jnp.dot(newton.T, gram_full[:, :NRHS], precision=highest)
    scales = lax.rsqrt(jnp.diagonal(image) + EPSILON)
    scaled = image * scales[:, None] * scales[None, :]
    factor = jnp.linalg.cholesky(scaled)
    coeffs = scales[:, None] * jax.scipy.linalg.cho_solve(
        (factor, True), scales[:, None] * right_side
    )
    initial_sq = jnp.diagonal(gram_full)[:NRHS]
    estimate = (initial_sq - jnp.sum(right_side * coeffs, axis=0)) / initial_sq
    return (coeffs, jnp.dot(newton, coeffs, precision=highest), estimate)


def body(residual_block, diagonal):
    highest = lax.Precision.HIGHEST
    width_rhs, cells_x, cells_y, cells_z = residual_block.shape
    total_x = cells_x * lax.axis_size("gx")
    total_y = cells_y * lax.axis_size("gy")
    powers = [residual_block]
    depth = len(SHIFTS)
    outgoing = jnp.concatenate([residual_block, diagonal[None]], 0)
    extended = padded_2(outgoing, (("gx", 1), ("gy", 2)), depth)
    field_now = extended[:width_rhs]
    diag_wide = extended[width_rhs]
    coord_x = (
        lax.axis_index("gx") * cells_x - depth + jnp.arange(cells_x + 2 * depth, dtype=jnp.int32)
    )
    coord_y = (
        lax.axis_index("gy") * cells_y - depth + jnp.arange(cells_y + 2 * depth, dtype=jnp.int32)
    )
    inside_x = (coord_x >= 0) & (coord_x < total_x)
    inside_y = (coord_y >= 0) & (coord_y < total_y)
    for step_index, shift_now in enumerate(SHIFTS):
        margin = depth - 1 - step_index
        lower = depth - margin
        span_x = cells_x + 2 * margin
        span_y = cells_y + 2 * margin
        diag_now = diag_wide[lower : lower + span_x, lower : lower + span_y]
        field_now = apply_padded(field_now, diag_now, shift_now)
        inside = (
            inside_x[lower : lower + span_x][:, None] & inside_y[lower : lower + span_y][None, :]
        )
        field_now = jnp.where(inside[None, :, :, None], field_now, 0.0)
        powers.append(field_now[:, margin : margin + cells_x, margin : margin + cells_y])
    basis = jnp.concatenate(powers, 0).reshape(len(powers) * width_rhs, -1)
    local_gram = lax.dot_general(
        basis,
        basis,
        (((1,), (1,)), ((), ())),
        precision=highest,
        preferred_element_type=jnp.float32,
    )
    gram_full = lax.psum(local_gram, ("gx", "gy"))
    coeffs, combined, estimate = solve_small(gram_full)
    kept = len(SHIFTS) * width_rhs
    correction = lax.dot_general(
        coeffs,
        basis[:kept],
        (((0,), (0,)), ((), ())),
        precision=highest,
        preferred_element_type=jnp.float32,
    )
    removed = lax.dot_general(
        combined,
        basis,
        (((0,), (0,)), ((), ())),
        precision=highest,
        preferred_element_type=jnp.float32,
    )
    new_residual = residual_block - removed.reshape(residual_block.shape)
    return (correction.reshape(residual_block.shape), new_residual, estimate)


def solution(mesh):
    in_specs = (P(None, "gx", "gy", None), P("gx", "gy", None))
    out_specs = (P(None, "gx", "gy", None), P(None, "gx", "gy", None), P())
    return jax.shard_map(body, mesh=mesh, in_specs=in_specs, out_specs=out_specs, check_vma=False)
```

profile of v0, /device:TPU:0, one launch (start us, length us, event | category | flops | bytes accessed | tf_op | source)
XLA Modules:
  0.0 107.6 jit_solution(6671456844812418066)
XLA Ops:
  0.6 1.1 %constant_dynamic-update-slice_fusion.4 = (f32[40,4,8,256]{3,0,2,1:T(8,128)S(1)}, f32[9,4,8,256]{3,0,2,1:T(8,128)S(1)}, f32[8,4,8,256]{3,0,2,1:T(8,128)S(1)}) fusion(f32[8,4,8,256]{3,2,1,0:T(8,128)} %param.3), kind=kLoop, calls=%fused_computation.97 | loop fusion | bytes 1048576
  1.8 0.8 broadcast_in_dim.59
  2.7 1.3 %collective-permute-start.1 = (f32[9,4,8,256]{3,0,2,1:T(8,128)S(1)}, f32[9,4,8,256]{3,0,2,1:T(8,128)S(1)}, u32[]{:S(2)}, u32[]{:S(2)}) collective-permute-start(f32[9,4,8,256]{3,0,2,1:T(8,128)S(1)} %dynamic-update-slice.9), channel_id=1, source_target_pairs={{4,0},{8,4},{12,8},{16,12},{20,16},{24,20},{28,24},{5,1},{9,5},{13... | collective-permute-start | bytes 884744 | tf_op jit(solution)/shard_map/ppermute | solution.py:27
  4.0 5.6 %collective-permute-start = (f32[9,4,8,256]{3,0,2,1:T(8,128)S(1)}, f32[9,4,8,256]{3,0,2,1:T(8,128)S(1)}, u32[]{:S(2)}, u32[]{:S(2)}) collective-permute-start(f32[9,4,8,256]{3,0,2,1:T(8,128)S(1)} %dynamic-update-slice.9), channel_id=1, source_target_pairs={{0,4},{4,8},{8,12},{12,16},{16,20},{20,24},{24,28},{1,5},{5,9},{9,... | collective-permute-start | bytes 884744 | tf_op jit(solution)/shard_map/ppermute | solution.py:24
  10.4 9.2 %collective-permute-done.1 = f32[9,4,8,256]{3,0,2,1:T(8,128)S(1)} collective-permute-done((f32[9,4,8,256]{3,0,2,1:T(8,128)S(1)}, f32[9,4,8,256]{3,0,2,1:T(8,128)S(1)}, u32[]{:S(2)}, u32[]{:S(2)}) %collective-permute-start.1) | collective-permute-done | bytes 294944 | tf_op jit(solution)/shard_map/ppermute | solution.py:27
  19.5 11.4 %collective-permute-done = f32[9,4,8,256]{3,0,2,1:T(8,128)S(1)} collective-permute-done((f32[9,4,8,256]{3,0,2,1:T(8,128)S(1)}, f32[9,4,8,256]{3,0,2,1:T(8,128)S(1)}, u32[]{:S(2)}, u32[]{:S(2)}) %collective-permute-start) | collective-permute-done | bytes 294944 | tf_op jit(solution)/shard_map/ppermute | solution.py:24
  31.5 1.3 %collective-permute-start.3 = (f32[9,12,4,256]{3,2,1,0:T(4,128)S(1)}, f32[9,12,4,256]{3,2,1,0:T(4,128)S(1)}, u32[]{:S(2)}, u32[]{:S(2)}) collective-permute-start(f32[9,12,4,256]{3,2,1,0:T(4,128)S(1)} %copy.26), channel_id=1, source_target_pairs={{1,0},{2,1},{3,2},{5,4},{6,5},{7,6},{9,8},{10,9},{11,10},{13,12},{... | collective-permute-start | bytes 1327112 | tf_op jit(solution)/shard_map/ppermute | solution.py:27
  33.1 3.1 %collective-permute-start.2 = (f32[9,12,4,256]{3,2,1,0:T(4,128)S(1)}, f32[9,12,4,256]{3,2,1,0:T(4,128)S(1)}, u32[]{:S(2)}, u32[]{:S(2)}) collective-permute-start(f32[9,12,4,256]{3,2,1,0:T(4,128)S(1)} %copy.25), channel_id=1, source_target_pairs={{0,1},{1,2},{2,3},{4,5},{5,6},{6,7},{8,9},{9,10},{10,11},{12,13},{... | collective-permute-start | bytes 1327112 | tf_op jit(solution)/shard_map/ppermute | solution.py:24
  36.6 0.9 collective-permute-done.2
  38.3 0.9 fusion.2
  39.4 0.8 fusion.17
  40.2 0.7 fusion.12
  42.5 1.2 %convolution_bitcast_fusion = f32[40,40]{1,0:T(8,128)S(1)} fusion(f32[40,4,8,256]{3,0,2,1:T(8,128)S(1)} %get-tuple-element.18), kind=kOutput, calls=%fused_computation.32 | convolution fusion | flops 157286400 | bytes 1317120 | tf_op jit(solution)/shard_map/dot_general | solution.py:100
  43.7 47.7 %psum.7 = f32[40,40]{1,0:T(8,128)S(1)} all-reduce(f32[40,40]{1,0:T(8,128)S(1)} %convolution_bitcast_fusion), channel_id=1, replica_groups=mesh['gx'=8,'gy'=4] {'gx','gy'}, use_global_device_ids=true, to_apply=%region_0.1 | all-reduce | flops 1600 | bytes 12800 | tf_op jit(solution)/shard_map/psum | solution.py:107
  92.8 0.7 gather_fusion
  93.6 2.9 %cholesky.16 = f32[32,32]{1,0:T(8,128)S(1)} custom-call(f32[32,32]{1,0:T(8,128)S(1)} %add_multiply_fusion), custom_call_target="Cholesky" | custom-call | tf_op jit(solution)/shard_map/jit(cholesky)/cholesky | solution.py:59
  96.6 0.6 compare_reduce_fusion
  97.2 0.7 fusion.50
  97.9 2.4 %custom-call.10 = f32[1,32,32]{1,2,0:T(8,128)S(1)} custom-call(f32[1,32,32]{2,1,0:T(8,128)S(1)} %fusion.50), custom_call_target="InvertDiagBlocksLowerTriangular" | custom-call | tf_op jit(solution)/shard_map/jit(_cho_solve)/triangular_solve | solution.py:60
  100.9 1.2 %fusion.18 = f32[8,4,8,256]{3,0,2,1:T(8,128)S(1)} fusion(f32[4,8,256,32]{2,1,0,3:T(8,128)S(1)} %bitcast.67, f32[32,8]{0,1:T(8,128)S(1)} %get-tuple-element.24), kind=kOutput, calls=%fused_computation.36 | convolution fusion | flops 25165824 | bytes 1311744 | tf_op jit(solution)/shard_map/dot_general | solution.py:110
  102.1 0.8 copy.37
  103.8 1.5 %fusion.7 = f32[8,4,8,256]{3,0,2,1:T(8,128)S(1)} fusion(f32[8,40,1,1]{1,0,3,2:T(8,128)S(1)} %convolution_bitcast_fusion.1, f32[4,8,256,40]{2,1,0,3:T(8,128)S(1)} %bitcast.66, f32[8,4,8,256]{3,2,1,0:T(8,128)S(1)} %copy-done), kind=kOutput, calls=%fused_computation.21 | convolution fusion | flops 31522816 | bytes 1836288 | tf_op jit(solution)/shard_map/dot_general | solution.py:117
  105.3 0.8 copy.38
  106.1 1.0 gather_fusion.1
  (61 shorter events, 8.2 us)
Async XLA Ops:
  2.7 16.8 %collective-permute-start.1 = (f32[9,4,8,256]{3,0,2,1:T(8,128)S(1)}, f32[9,4,8,256]{3,0,2,1:T(8,128)S(1)}, u32[]{:S(2)}, u32[]{:S(2)}) collective-permute-start(f32[9,4,8,256]{3,0,2,1:T(8,128)S(1)} %dynamic-update-slice.9), channel_id=1, source_target_pairs={{4,0},{8,4},{12,8},{16,12},{20,16},{24,20},{28,24},{5,1},{9,5},{13... | collective-permute-start | bytes 884744 | tf_op jit(solution)/shard_map/ppermute | solution.py:27
  4.0 26.9 %collective-permute-start = (f32[9,4,8,256]{3,0,2,1:T(8,128)S(1)}, f32[9,4,8,256]{3,0,2,1:T(8,128)S(1)}, u32[]{:S(2)}, u32[]{:S(2)}) collective-permute-start(f32[9,4,8,256]{3,0,2,1:T(8,128)S(1)} %dynamic-update-slice.9), channel_id=1, source_target_pairs={{0,4},{4,8},{8,12},{12,16},{16,20},{20,24},{24,28},{1,5},{5,9},{9,... | collective-permute-start | bytes 884744 | tf_op jit(solution)/shard_map/ppermute | solution.py:24
  31.5 4.8 %collective-permute-start.3 = (f32[9,12,4,256]{3,2,1,0:T(4,128)S(1)}, f32[9,12,4,256]{3,2,1,0:T(4,128)S(1)}, u32[]{:S(2)}, u32[]{:S(2)}) collective-permute-start(f32[9,12,4,256]{3,2,1,0:T(4,128)S(1)} %copy.26), channel_id=1, source_target_pairs={{1,0},{2,1},{3,2},{5,4},{6,5},{7,6},{9,8},{10,9},{11,10},{13,12},{... | collective-permute-start | bytes 1327112 | tf_op jit(solution)/shard_map/ppermute | solution.py:27
  33.1 4.4 %collective-permute-start.2 = (f32[9,12,4,256]{3,2,1,0:T(4,128)S(1)}, f32[9,12,4,256]{3,2,1,0:T(4,128)S(1)}, u32[]{:S(2)}, u32[]{:S(2)}) collective-permute-start(f32[9,12,4,256]{3,2,1,0:T(4,128)S(1)} %copy.25), channel_id=1, source_target_pairs={{0,1},{1,2},{2,3},{4,5},{5,6},{6,7},{8,9},{9,10},{10,11},{12,13},{... | collective-permute-start | bytes 1327112 | tf_op jit(solution)/shard_map/ppermute | solution.py:24
  42.5 48.9 %copy-start.1 = (f32[40,32]{1,0:T(8,128)S(1)}, f32[40,32]{1,0:T(8,128)}, u32[]{:S(2)}) copy-start(f32[40,32]{1,0:T(8,128)} %constant.132.clone) | copy-start | bytes 15364
  102.8 0.9 copy-start
where the time goes:
time: 108 us
  blocking collectives  47.7 us (44%)
  waiting for transfers between devices  21.5 us (20%)
  other arithmetic  12.3 us (11%)
  starting transfers between devices  11.2 us (10%)
  local copies, waits for them, and re-layouts  8.91 us (8%)
  matrix products  4.96 us (5%)
    psum x1, blocking collectives, body(): gram_full = lax.psum(local_gram, ('gx', 'gy'))  47.7 us
    ppermute x2, waiting for transfers between devices, padded_2(): lax.ppermute(lax.slice_in_dim(block, block.shape[dim] - width, None, axis...  12.3 us
    ppermute x2, waiting for transfers between devices, padded_2(): lax.ppermute(lax.slice_in_dim(block, 0, width, axis=dim), axis, backward)  9.16 us
    ppermute x2, starting transfers between devices, padded_2(): lax.ppermute(lax.slice_in_dim(block, block.shape[dim] - width, None, axis...  8.62 us
    unnamed x13, local copies, waits for them, and re-layouts  4.37 us
    another operation x3, other arithmetic, solve_small(): factor = jnp.linalg.cholesky(scaled)  3.6 us
    another operation x2, other arithmetic, solve_small(): jax.scipy.linalg.cho_solve((factor, True), scales[:, None] * right_side)  3.09 us
    ppermute x2, starting transfers between devices, padded_2(): lax.ppermute(lax.slice_in_dim(block, 0, width, axis=dim), axis, backward)  2.58 us
  transfers between devices with their start and end apart: 4, of which 3 were waited for; matrix products, arithmetic and copies ran while one was open for 1% of the time, Pallas kernels for 0%

commit v1 on v0

v1 whole, which is shorter than its diff:
```python
import functools

import jax
import jax.numpy as jnp
from jax import lax
from jax.experimental import pallas as pl
from jax.experimental.pallas import tpu as pltpu
from jax.sharding import PartitionSpec as P

WEIGHT_X = 0.4
WEIGHT_Y = 0.2
WEIGHT_Z = 0.1
CENTRE = 2.2
SCALE_POWER = 3.0
SHIFTS = (6.0, 1.5, 4.5, 3.0)
EPSILON = 1e-06
DEPTH = len(SHIFTS)
MESH = pl.DeviceIdType.MESH
LANES = 128


def kernel(nx, ny, dims, r_ref, d_ref, corr_ref, new_ref, est_ref,
           e_bufs, sy, dd, basis, gram, gather_y, gather_x, wide, halo_send, halo_recv, red_send_y, red_recv_y,
           red_send_x, red_recv_x):
    nf, cx, cy, nz = dims
    dep = DEPTH
    nb = (dep + 1) * nf
    nk = dep * nf
    gx = lax.axis_index("gx")
    gy = lax.axis_index("gy")
    e0 = e_bufs.at[0]
    wx, wy = cx + 2 * dep, cy + 2 * dep
    nt = nz // LANES

    barrier = pltpu.get_barrier_semaphore()
    for k in range(1, nx):
        pl.semaphore_signal(barrier, inc=1, device_id=(lax.rem(gx + k, nx), gy), device_id_type=MESH)
    for k in range(1, ny):
        pl.semaphore_signal(barrier, inc=1, device_id=(gx, lax.rem(gy + k, ny)), device_id_type=MESH)

    for x in range(cx):
        for y in range(cy):
            v = jnp.concatenate([r_ref[pl.ds((x * nt + t) * cy + y, nf, stride=cx * cy * nt), :] for t in range(nt)], 1)
            e0[dep + x, dep + y] = v
            cell = x * cy + y
            basis[0:nf, cell * nz:(cell + 1) * nz] = v
        dd[dep + x, 1] = d_ref[x]

    zero_row = jnp.zeros((dep, cy, nf, nz), jnp.float32)
    zero_col = jnp.zeros((dep, nf, nz), jnp.float32)

    def clear_rows(lo):
        def one(i, c):
            e0[lo + i, dep:dep + cy] = zero_row[0]
            dd[lo + i, 1] = jnp.zeros((cy, nz), jnp.float32)
            return c
        lax.fori_loop(0, dep, one, 0)

    def clear_cols(lo, tile):
        def one(i, c):
            e0[i, lo:lo + dep] = zero_col
            dd[i, tile] = jnp.zeros((cy, nz), jnp.float32)
            return c
        lax.fori_loop(0, wx, one, 0)

    pl.when(gx == 0)(lambda: clear_rows(0))
    pl.when(gx == nx - 1)(lambda: clear_rows(dep + cx))
    pl.when(gy == 0)(lambda: clear_cols(0, 0))
    pl.when(gy == ny - 1)(lambda: clear_cols(dep + cy, 2))

    pl.semaphore_wait(barrier, nx + ny - 2)

    def copy(src, dst, slot, dev):
        return pltpu.make_async_remote_copy(src_ref=src, dst_ref=dst, send_sem=halo_send.at[slot],
                                            recv_sem=halo_recv.at[slot], device_id=dev, device_id_type=MESH)

    own_y = pl.ds(dep, cy)
    up_rows, down_rows = pl.ds(cx, dep), pl.ds(dep, dep)
    up = (gx + 1, gy)
    down = (gx - 1, gy)
    has_up, has_down = gx < nx - 1, gx > 0
    up_copies = [copy(e0.at[up_rows, own_y], e0.at[pl.ds(0, dep), own_y], 0, up),
                 copy(dd.at[up_rows, 1], dd.at[pl.ds(0, dep), 1], 1, up)]
    down_copies = [copy(e0.at[down_rows, own_y], e0.at[pl.ds(dep + cx, dep), own_y], 2, down),
                   copy(dd.at[down_rows, 1], dd.at[pl.ds(dep + cx, dep), 1], 3, down)]

    right, left = (gx, gy + 1), (gx, gy - 1)
    has_right, has_left = gy < ny - 1, gy > 0
    groups = [pl.ds(dep, cx), pl.ds(0, dep), pl.ds(dep + cx, dep)]
    right_copies, left_copies = [], []
    for i, rows in enumerate(groups):
        right_copies.append([copy(e0.at[rows, pl.ds(cy, dep)], e0.at[rows, pl.ds(0, dep)], 4 + 4 * i, right),
                             copy(dd.at[rows, 1], dd.at[rows, 0], 5 + 4 * i, right)])
        left_copies.append([copy(e0.at[rows, pl.ds(dep, dep)], e0.at[rows, pl.ds(dep + cy, dep)], 6 + 4 * i, left),
                            copy(dd.at[rows, 1], dd.at[rows, 2], 7 + 4 * i, left)])

    def start(pred, copies):
        @pl.when(pred)
        def _():
            for c in copies:
                c.start()

    def wait_recv(pred, copies):
        @pl.when(pred)
        def _():
            for c in copies:
                c.wait_recv()

    def wait_send(pred, copies):
        @pl.when(pred)
        def _():
            for c in copies:
                c.wait_send()

    start(has_up, up_copies)
    start(has_down, down_copies)
    start(has_right, right_copies[0])
    start(has_left, left_copies[0])
    wait_recv(has_down, up_copies)
    start(has_right, right_copies[1])
    start(has_left, left_copies[1])
    wait_recv(has_up, down_copies)
    start(has_right, right_copies[2])
    start(has_left, left_copies[2])
    for i in range(3):
        wait_recv(has_left, right_copies[i])
        wait_recv(has_right, left_copies[i])

    lane = lax.broadcasted_iota(jnp.int32, (nf, nz), 1)
    first, last = lane == 0, lane == nz - 1

    def sum_z(v):
        lo = jnp.where(first, 0.0, pltpu.roll(v, 1, 1))
        hi = jnp.where(last, 0.0, pltpu.roll(v, nz - 1, 1))
        return v + WEIGHT_Z * (lo + hi)

    total_x, total_y = cx * nx, cy * ny
    for j, shift in enumerate(SHIFTS):
        src = e_bufs.at[j]
        def row_pass(x, c, src=src, j=j):
            prev = sum_z(src[x, j])
            here = sum_z(src[x, j + 1])
            for y in range(j + 1, wy - j - 1):
                nxt = sum_z(src[x, y + 1])
                sy[x, y] = here + WEIGHT_Y * (prev + nxt)
                prev, here = here, nxt
            return c
        lax.fori_loop(j, wx - j, row_pass, 0)

        def col_pass(x, c, src=src, j=j, shift=shift, keep=False):
            at_x = gx * cx + x - dep
            in_x = (at_x >= 0) & (at_x < total_x)
            for y in range(j + 1, wy - j - 1):
                at_y = gy * cy + y - dep
                factor = jnp.where(in_x & (at_y >= 0) & (at_y < total_y), 1.0 / SCALE_POWER, 0.0)
                tile, sub = (y - dep + cy) // cy, (y - dep) % cy
                diag = dd[x, tile, sub:sub + 1, :]
                centre = src[x, y]
                s = sy[x, y] + WEIGHT_X * (sy[x - 1, y] + sy[x + 1, y])
                v = ((CENTRE + 1.0 - shift + diag) * centre - s) * factor
                if j + 1 < dep:
                    e_bufs[j + 1, x, y] = v
                if keep and dep <= y < dep + cy:
                    cell = (x - dep) * cy + (y - dep)
                    basis[(j + 1) * nf:(j + 2) * nf, pl.ds(pl.multiple_of(cell * nz, nz), nz)] = v
            return c
        if j + 1 < dep:
            lax.fori_loop(j + 1, dep, col_pass, 0)
            lax.fori_loop(dep + cx, wx - j - 1, col_pass, 0)
        lax.fori_loop(dep, dep + cx, functools.partial(col_pass, keep=True), 0)

    b = basis[...]
    local = lax.dot_general(b, b, (((1,), (1,)), ((), ())), precision=lax.Precision.HIGHEST,
                            preferred_element_type=jnp.float32)
    gram[...] = jnp.zeros_like(gram)
    gram[:, 0:nb] = local

    def reduce(buf, value, me, n, send, recv, dev):
        buf[me] = value
        copies = []
        for k in range(1, n):
            to = lax.rem(me + k, n)
            c = pltpu.make_async_remote_copy(src_ref=buf.at[me], dst_ref=buf.at[me], send_sem=send.at[k],
                                             recv_sem=recv.at[k], device_id=dev(to), device_id_type=MESH)
            c.start()
            copies.append(c)
        for k in range(1, n):
            frm = lax.rem(me - k + n, n)
            pltpu.make_async_remote_copy(src_ref=buf.at[frm], dst_ref=buf.at[frm], send_sem=send.at[k],
                                         recv_sem=recv.at[k], device_id=dev(frm), device_id_type=MESH).wait_recv()
        total = buf[0]
        for k in range(1, n):
            total = total + buf[k]
        return total, copies

    part, copies_y = reduce(gather_y, gram[...], gy, ny, red_send_y, red_recv_y, lambda t: (gx, t))
    full, copies_x = reduce(gather_x, part, gx, nx, red_send_x, red_recv_x, lambda t: (t, gy))

    lane_b = lax.broadcasted_iota(jnp.int32, (nb, LANES), 1)
    sigma_lane = jnp.zeros((nb, LANES), jnp.float32)
    for j, shift in enumerate(SHIFTS):
        sigma_lane = jnp.where((lane_b >= j * nf) & (lane_b < (j + 1) * nf), shift, sigma_lane)
    gn = full * sigma_lane + SCALE_POWER * pltpu.roll(full, LANES - nf, 1)

    def newton_rows(m):
        return jnp.concatenate([SHIFTS[j] * m[j * nf:(j + 1) * nf] + SCALE_POWER * m[(j + 1) * nf:(j + 2) * nf]
                                for j in range(dep)], 0)

    image = newton_rows(gn)
    right_side = pltpu.roll(newton_rows(full), nk, 1)
    lane_k = lax.broadcasted_iota(jnp.int32, (nk, LANES), 1)
    row_k = lax.broadcasted_iota(jnp.int32, (nk, LANES), 0)
    on_diag = jnp.where(lane_k == row_k, image, 0.0)
    s_col = lax.rsqrt(jnp.sum(on_diag, axis=1, keepdims=True) + EPSILON)
    s_row = lax.rsqrt(jnp.sum(on_diag, axis=0, keepdims=True) + EPSILON)
    in_image = lane_k < nk
    in_right = (lane_k >= nk) & (lane_k < nk + nf)
    m = jnp.where(in_image, image * s_col * s_row, jnp.where(in_right, right_side * s_col, 0.0))
    for k in range(nk):
        row = m[k:k + 1, :]
        row = row / row[:, k:k + 1]
        m = jnp.where(row_k == k, row, m - m[:, k:k + 1] * row)
    coeffs = jnp.where(in_right, m * s_col, 0.0)

    diag0 = jnp.sum(jnp.where(lane_k[:nf] == row_k[:nf], full[:nf], 0.0), axis=0, keepdims=True)
    used = pltpu.roll(jnp.sum(jnp.where(in_right, right_side * coeffs, 0.0), axis=0, keepdims=True), LANES - nk, 1)
    est_ref[...] = (diag0 - used) / jnp.where(lane_k[:1] < nf, diag0, 1.0)

    blocks = [coeffs[j * nf:(j + 1) * nf] for j in range(dep)]
    combined = [SHIFTS[0] * blocks[0]]
    for j in range(1, dep):
        combined.append(SHIFTS[j] * blocks[j] + SCALE_POWER * blocks[j - 1])
    combined.append(SCALE_POWER * blocks[dep - 1])
    wide[...] = jnp.zeros_like(wide)
    for j in range(dep + 1):
        moved = pltpu.roll(combined[j], nf, 1)
        wide[j * nf:(j + 1) * nf, :] = moved + blocks[j] if j < dep else moved
    weights = jnp.transpose(wide[...])[nk:nk + 2 * nf, 0:nb]
    out = lax.dot_general(weights, basis[...], (((1,), (0,)), ((), ())), precision=lax.Precision.HIGHEST,
                          preferred_element_type=jnp.float32)
    for cell in range(cx * cy):
        x, y = cell // cy, cell % cy
        for t in range(nt):
            span = slice(cell * nz + t * LANES, cell * nz + (t + 1) * LANES)
            rows = pl.ds((x * nt + t) * cy + y, nf, stride=cx * cy * nt)
            corr_ref[rows, :] = out[0:nf, span]
            new_ref[rows, :] = basis[0:nf, span] - out[nf:2 * nf, span]

    wait_send(has_up, up_copies)
    wait_send(has_down, down_copies)
    for i in range(3):
        wait_send(has_right, right_copies[i])
        wait_send(has_left, left_copies[i])
    for c in copies_y + copies_x:
        c.wait_send()


def solution(mesh):
    nx, ny = mesh.shape["gx"], mesh.shape["gy"]

    def body(residual_block, diagonal):
        nf, cx, cy, nz = residual_block.shape
        nb = (DEPTH + 1) * nf
        wx, wy = cx + 2 * DEPTH, cy + 2 * DEPTH
        nt = nz // LANES
        flat = jax.ShapeDtypeStruct((nf * cx * nt * cy, LANES), jnp.float32)

        def tiles(v):
            return v.reshape(nf, cx, cy, nt, LANES).transpose(0, 1, 3, 2, 4).reshape(flat.shape)

        def untile(v):
            return v.reshape(nf, cx, nt, cy, LANES).transpose(0, 1, 3, 2, 4).reshape(nf, cx, cy, nz)

        vmem = pl.BlockSpec(memory_space=pltpu.VMEM)
        corr, new, est = pl.pallas_call(
            functools.partial(kernel, nx, ny, (nf, cx, cy, nz)),
            out_shape=(flat, flat, jax.ShapeDtypeStruct((1, LANES), jnp.float32)),
            in_specs=[vmem, vmem],
            out_specs=(vmem, vmem, vmem),
            scratch_shapes=[
                pltpu.VMEM((DEPTH, wx, wy, nf, nz), jnp.float32),
                pltpu.VMEM((wx, wy, nf, nz), jnp.float32),
                pltpu.VMEM((wx, 3, cy, nz), jnp.float32),
                pltpu.VMEM((nb, cx * cy * nz), jnp.float32),
                pltpu.VMEM((nb, LANES), jnp.float32),
                pltpu.VMEM((ny, nb, LANES), jnp.float32),
                pltpu.VMEM((nx, nb, LANES), jnp.float32),
                pltpu.VMEM((LANES, LANES), jnp.float32),
                pltpu.SemaphoreType.DMA((16,)),
                pltpu.SemaphoreType.DMA((16,)),
                pltpu.SemaphoreType.DMA((ny,)),
                pltpu.SemaphoreType.DMA((ny,)),
                pltpu.SemaphoreType.DMA((nx,)),
                pltpu.SemaphoreType.DMA((nx,)),
            ],
            compiler_params=pltpu.CompilerParams(collective_id=0, has_side_effects=True),
        )(tiles(residual_block), diagonal)
        return untile(corr), untile(new), est[0, :nf]

    return jax.shard_map(body, mesh=mesh, in_specs=(P(None, "gx", "gy", None), P("gx", "gy", None)),
                         out_specs=(P(None, "gx", "gy", None), P(None, "gx", "gy", None), P()), check_vma=False)
```

time: 108 us -> 49.9 us (0.46)
  blocking collectives: 47.7 us -> 0 us
  Pallas kernels: 0 us -> 45.5 us
  waiting for transfers between devices: 21.5 us -> 0 us
  other arithmetic: 12.3 us -> 0 us
  starting transfers between devices: 11.2 us -> 0 us
  local copies, waits for them, and re-layouts: 8.91 us -> 3.56 us
  matrix products: 4.96 us -> 0 us
    psum x1 -> x0, blocking collectives: 47.7 us -> none  [body(): gram_full = lax.psum(local_gram, ('gx', 'gy'))]
    pallas_call x0 -> x1, Pallas kernels: none -> 45.5 us  [body(): pl.pallas_call(functools.partial(kernel, nx, ny, (nf, cx, cy, nz)), out_s...]
    ppermute x4 -> x0, waiting for transfers between devices: 21.5 us -> none  [the longest x2 12.3 us: padded_2(): lax.ppermute(lax.slice_in_dim(block, block.shape[dim] - width, None, axis...]
    ppermute x4 -> x0, starting transfers between devices: 11.2 us -> none  [the longest x2 8.62 us: padded_2(): lax.ppermute(lax.slice_in_dim(block, block.shape[dim] - width, None, axis...]
    another operation x5 -> x0, other arithmetic: 6.68 us -> none  [the longest x3 3.6 us: solve_small(): factor = jnp.linalg.cholesky(scaled)]
    dot_general x7 -> x0, matrix products: 4.54 us -> none  [the longest x1 1.5 us: body(): lax.dot_general(combined, basis, (((0,), (0,)), ((), ())), precision=high...]
    add x8 -> x0, other arithmetic: 2.71 us -> none  [the longest x4 2.33 us: apply_padded(): sum_z = padded + WEIGHT_Z * (along_z[..., :-2] + along_z[..., 2:])]
    gather x2 -> x0, local copies, waits for them, and re-layouts: 1.69 us -> none  [the longest x1 0.95 us: solve_small(): initial_sq = jnp.diagonal(gram_full)[:NRHS]]
  transfers between devices with their start and end apart: 4 -> 0, of which waited for: 3 -> 0; matrix products, arithmetic and copies ran while one was open for 1% -> 0% of each run, Pallas kernels for 0% -> 0%
where the time goes in v1:
time: 49.9 us; the launch traced here: 49.7 us
  Pallas kernels  45.5 us (91%)
  local copies, waits for them, and re-layouts  3.56 us (7%)
  between operations  0.65 us (1%)
    pallas_call x1, Pallas kernels, body(): pl.pallas_call(functools.partial(kernel, nx, ny, (nf, cx, cy, nz)), out_s...  45.5 us
    unnamed x6, local copies, waits for them, and re-layouts  3.05 us

profile of v1, /device:TPU:0, one launch (start us, length us, event | category | flops | bytes accessed | tf_op | source)
XLA Modules:
  0.0 49.7 jit_solution(9997697654255693053)
XLA Ops:
  0.6 45.5 %shard_map.49 = (f32[512,128]{1,0:T(8,128)}, f32[512,128]{1,0:T(8,128)}, f32[1,128]{1,0:T(1,128)}) custom-call(f32[512,128]{1,0:T(8,128)} %bitcast.17, f32[4,8,256]{2,1,0:T(8,128)} %d_ref.1), custom_call_target="tpu_custom_call" | custom-call | tf_op jit(solution)/shard_map/pallas_call | solution.py:275
  46.2 0.0 copy-start.1
  46.2 0.6 %copy-done.1 = f32[1,128]{1,0:T(1,128)S(1)} copy-done((f32[1,128]{1,0:T(1,128)S(1)}, f32[1,128]{1,0:T(1,128)}, u32[]{:S(2)}) %copy-start.1) | copy-done | bytes 536
  46.8 0.5 %slice_bitcast_fusion = f32[8]{0:T(128)} fusion(f32[1,128]{1,0:T(1,128)S(1)} %copy-done.1), kind=kLoop, calls=%fused_computation | loop fusion | bytes 64 | tf_op jit(solution)/shard_map/squeeze | solution.py:298
  47.3 0.0 copy-start
  47.3 1.7 %copy.7 = f32[8,4,8,256]{3,2,1,0:T(8,128)} copy(f32[8,4,8,256]{3,2,1,0:T(8,128)} %bitcast.19) | data formatting | bytes 524288
  49.0 0.0 copy-done
  49.0 0.7 %copy.8 = f32[8,4,8,256]{3,2,1,0:T(8,128)} copy(f32[8,4,8,256]{3,2,1,0:T(8,128)S(1)} %bitcast.18) | data formatting | bytes 524288
Async XLA Ops:
  46.2 0.6 %copy-start.1 = (f32[1,128]{1,0:T(1,128)S(1)}, f32[1,128]{1,0:T(1,128)}, u32[]{:S(2)}) copy-start(f32[1,128]{1,0:T(1,128)} %get-tuple-element.8) | copy-start | bytes 1540
  47.3 1.7 %copy-start = (f32[512,128]{1,0:T(8,128)S(1)}, f32[512,128]{1,0:T(8,128)}, u32[]{:S(2)}) copy-start(f32[512,128]{1,0:T(8,128)} %get-tuple-element.7) | copy-start | bytes 786436

commit v2 on v1

--- a/solution.py
+++ b/solution.py
@@ -46,25 +46,30 @@
             basis[0:nf, cell * nz:(cell + 1) * nz] = v
         dd[dep + x, 1] = d_ref[x]
 
-    zero_row = jnp.zeros((dep, cy, nf, nz), jnp.float32)
-    zero_col = jnp.zeros((dep, nf, nz), jnp.float32)
-
-    def clear_rows(lo):
+    even = lax.rem(gx, 2) == 0
+    partner = jnp.where(even, gx + 1, gx - 1)
+    beyond = jnp.where(even, gx + 2, gx - 2)
+    can_forward = (beyond >= 0) & (beyond < nx)
+    gets_forward = (gx > 0) & (gx < nx - 1)
+    has_right, has_left = gy < ny - 1, gy > 0
+    near = jnp.where(even, dep + cx, 0)
+    far = jnp.where(even, 0, dep + cx)
+
+    @pl.when(jnp.logical_not(gets_forward))
+    def _():
         def one(i, c):
-            e0[lo + i, dep:dep + cy] = zero_row[0]
-            dd[lo + i, 1] = jnp.zeros((cy, nz), jnp.float32)
+            e0[far + i] = jnp.zeros((wy, nf, nz), jnp.float32)
+            dd[far + i] = jnp.zeros((3, cy, nz), jnp.float32)
             return c
         lax.fori_loop(0, dep, one, 0)
 
     def clear_cols(lo, tile):
         def one(i, c):
-            e0[i, lo:lo + dep] = zero_col
+            e0[i, lo:lo + dep] = jnp.zeros((dep, nf, nz), jnp.float32)
             dd[i, tile] = jnp.zeros((cy, nz), jnp.float32)
             return c
         lax.fori_loop(0, wx, one, 0)
 
-    pl.when(gx == 0)(lambda: clear_rows(0))
-    pl.when(gx == nx - 1)(lambda: clear_rows(dep + cx))
     pl.when(gy == 0)(lambda: clear_cols(0, 0))
     pl.when(gy == ny - 1)(lambda: clear_cols(dep + cy, 2))
 
@@ -75,56 +80,59 @@
                                             recv_sem=halo_recv.at[slot], device_id=dev, device_id_type=MESH)
 
     own_y = pl.ds(dep, cy)
-    up_rows, down_rows = pl.ds(cx, dep), pl.ds(dep, dep)
-    up = (gx + 1, gy)
-    down = (gx - 1, gy)
-    has_up, has_down = gx < nx - 1, gx > 0
-    up_copies = [copy(e0.at[up_rows, own_y], e0.at[pl.ds(0, dep), own_y], 0, up),
-                 copy(dd.at[up_rows, 1], dd.at[pl.ds(0, dep), 1], 1, up)]
-    down_copies = [copy(e0.at[down_rows, own_y], e0.at[pl.ds(dep + cx, dep), own_y], 2, down),
-                   copy(dd.at[down_rows, 1], dd.at[pl.ds(dep + cx, dep), 1], 3, down)]
-
-    right, left = (gx, gy + 1), (gx, gy - 1)
-    has_right, has_left = gy < ny - 1, gy > 0
-    groups = [pl.ds(dep, cx), pl.ds(0, dep), pl.ds(dep + cx, dep)]
-    right_copies, left_copies = [], []
-    for i, rows in enumerate(groups):
-        right_copies.append([copy(e0.at[rows, pl.ds(cy, dep)], e0.at[rows, pl.ds(0, dep)], 4 + 4 * i, right),
-                             copy(dd.at[rows, 1], dd.at[rows, 0], 5 + 4 * i, right)])
-        left_copies.append([copy(e0.at[rows, pl.ds(dep, dep)], e0.at[rows, pl.ds(dep + cy, dep)], 6 + 4 * i, left),
-                            copy(dd.at[rows, 1], dd.at[rows, 2], 7 + 4 * i, left)])
-
-    def start(pred, copies):
-        @pl.when(pred)
-        def _():
-            for c in copies:
-                c.start()
-
-    def wait_recv(pred, copies):
-        @pl.when(pred)
-        def _():
-            for c in copies:
-                c.wait_recv()
-
-    def wait_send(pred, copies):
-        @pl.when(pred)
-        def _():
-            for c in copies:
-                c.wait_send()
-
-    start(has_up, up_copies)
-    start(has_down, down_copies)
-    start(has_right, right_copies[0])
-    start(has_left, left_copies[0])
-    wait_recv(has_down, up_copies)
-    start(has_right, right_copies[1])
-    start(has_left, left_copies[1])
-    wait_recv(has_up, down_copies)
-    start(has_right, right_copies[2])
-    start(has_left, left_copies[2])
-    for i in range(3):
-        wait_recv(has_left, right_copies[i])
-        wait_recv(has_right, left_copies[i])
+    step = dep + 1
+    swap = [copy(dd.at[pl.ds(dep, cx), 1], dd.at[pl.ds(far, cx), 1], 0, (partner, gy))]
+    swap += [copy(e0.at[dep + i, own_y], e0.at[far + i, own_y], 1 + i, (partner, gy)) for i in range(cx)]
+    forward = [copy(dd.at[pl.ds(near, cx), 1], dd.at[pl.ds(far, cx), 1], step, (beyond, gy))]
+    forward += [copy(e0.at[near + i, own_y], e0.at[far + i, own_y], step + 1 + i, (beyond, gy)) for i in range(cx)]
+
+    def edges(rows, drows, slot, d_only=False):
+        right, left = (gx, gy + 1), (gx, gy - 1)
+        if d_only:
+            return (copy(dd.at[drows, 1], dd.at[drows, 0], slot, right),
+                    copy(dd.at[drows, 1], dd.at[drows, 2], slot + 1, left))
+        return (copy(e0.at[rows, pl.ds(cy, dep)], e0.at[rows, pl.ds(0, dep)], slot, right),
+                copy(e0.at[rows, pl.ds(dep, dep)], e0.at[rows, pl.ds(dep + cy, dep)], slot + 1, left))
+
+    base = 2 * step
+    own_edges = [edges(None, pl.ds(dep, cx), base, True), edges(pl.ds(dep, cx), None, base + 2)]
+    base += 4
+    near_edges = [edges(None, pl.ds(near, cx), base, True)]
+    near_edges += [edges(near + i, None, base + 2 + 2 * i) for i in range(cx)]
+    base += 2 * step
+    far_edges = [edges(None, pl.ds(far, cx), base, True)]
+    far_edges += [edges(far + i, None, base + 2 + 2 * i) for i in range(cx)]
+
+    def when(pred, act):
+        pl.when(pred)(act)
+
+    def start_edges(pair, pred=True):
+        when(has_right & pred, lambda: pair[0].start())
+        when(has_left & pred, lambda: pair[1].start())
+
+    def wait_edges(pairs, pred=True):
+        def low():
+            for pair in pairs:
+                pair[0].wait_recv()
+
+        def high():
+            for pair in pairs:
+                pair[1].wait_recv()
+        when(has_left & pred, low)
+        when(has_right & pred, high)
+
+    for c in swap:
+        c.start()
+    for pair in own_edges:
+        start_edges(pair)
+    for i in range(step):
+        swap[i].wait_recv()
+        when(can_forward, lambda i=i: forward[i].start())
+        start_edges(near_edges[i])
+
+    def take_far(i):
+        when(gets_forward, lambda: forward[i].wait_recv())
+        start_edges(far_edges[i], gets_forward)
 
     lane = lax.broadcasted_iota(jnp.int32, (nf, nz), 1)
     first, last = lane == 0, lane == nz - 1
@@ -135,39 +143,54 @@
         return v + WEIGHT_Z * (lo + hi)
 
     total_x, total_y = cx * nx, cy * ny
-    for j, shift in enumerate(SHIFTS):
+
+    def row_pass(j, x):
         src = e_bufs.at[j]
-        def row_pass(x, c, src=src, j=j):
-            prev = sum_z(src[x, j])
-            here = sum_z(src[x, j + 1])
-            for y in range(j + 1, wy - j - 1):
-                nxt = sum_z(src[x, y + 1])
-                sy[x, y] = here + WEIGHT_Y * (prev + nxt)
-                prev, here = here, nxt
+        prev = sum_z(src[x, j])
+        here = sum_z(src[x, j + 1])
+        for y in range(j + 1, wy - j - 1):
+            nxt = sum_z(src[x, y + 1])
+            sy[j, x, y] = here + WEIGHT_Y * (prev + nxt)
+            prev, here = here, nxt
+
+    def col_pass(j, x):
+        at_x = gx * cx + x - dep
+        in_x = (at_x >= 0) & (at_x < total_x)
+        for y in range(j + 1, wy - j - 1):
+            at_y = gy * cy + y - dep
+            factor = jnp.where(in_x & (at_y >= 0) & (at_y < total_y), 1.0 / SCALE_POWER, 0.0)
+            tile, sub = (y - dep + cy) // cy, (y - dep) % cy
+            diag = dd[x, tile, sub:sub + 1, :]
+            s = sy[j, x, y] + WEIGHT_X * (sy[j, x - 1, y] + sy[j, x + 1, y])
+            v = ((CENTRE + 1.0 - SHIFTS[j] + diag) * e_bufs[j, x, y] - s) * factor
+            if j + 1 < dep:
+                e_bufs[j + 1, x, y] = v
+            else:
+                cell = (x - dep) * cy + (y - dep)
+                basis[dep * nf:(dep + 1) * nf, pl.ds(pl.multiple_of(cell * nz, nz), nz)] = v
+
+    def sweep(one, j, lo, count):
+        def body(i, c):
+            one(j, lo + i)
             return c
-        lax.fori_loop(j, wx - j, row_pass, 0)
-
-        def col_pass(x, c, src=src, j=j, shift=shift, keep=False):
-            at_x = gx * cx + x - dep
-            in_x = (at_x >= 0) & (at_x < total_x)
-            for y in range(j + 1, wy - j - 1):
-                at_y = gy * cy + y - dep
-                factor = jnp.where(in_x & (at_y >= 0) & (at_y < total_y), 1.0 / SCALE_POWER, 0.0)
-                tile, sub = (y - dep + cy) // cy, (y - dep) % cy
-                diag = dd[x, tile, sub:sub + 1, :]
-                centre = src[x, y]
-                s = sy[x, y] + WEIGHT_X * (sy[x - 1, y] + sy[x + 1, y])
-                v = ((CENTRE + 1.0 - shift + diag) * centre - s) * factor
-                if j + 1 < dep:
-                    e_bufs[j + 1, x, y] = v
-                if keep and dep <= y < dep + cy:
-                    cell = (x - dep) * cy + (y - dep)
-                    basis[(j + 1) * nf:(j + 2) * nf, pl.ds(pl.multiple_of(cell * nz, nz), nz)] = v
-            return c
-        if j + 1 < dep:
-            lax.fori_loop(j + 1, dep, col_pass, 0)
-            lax.fori_loop(dep + cx, wx - j - 1, col_pass, 0)
-        lax.fori_loop(dep, dep + cx, functools.partial(col_pass, keep=True), 0)
+        if count > 0:
+            lax.fori_loop(0, count, body, 0)
+
+    wait_edges(own_edges)
+    wait_edges(near_edges)
+    take_far(0)
+    for j in range(dep):
+        lo = jnp.where(even, dep + j, j)
+        sweep(row_pass, j, lo, cx + dep - 2 * j)
+        sweep(col_pass, j, lo + 1, cx + dep - 2 - 2 * j)
+        take_far(1 + j)
+    wait_edges(far_edges, gets_forward)
+    for j in range(dep):
+        sweep(row_pass, j, jnp.where(even, j, cx + dep - j), dep)
+        sweep(col_pass, j, jnp.where(even, j + 1, cx + dep - 1 - j), dep)
+    for j in range(1, dep):
+        for cell in range(cx * cy):
+            basis[j * nf:(j + 1) * nf, cell * nz:(cell + 1) * nz] = e_bufs[j, dep + cell // cy, dep + cell % cy]
 
     b = basis[...]
     local = lax.dot_general(b, b, (((1,), (1,)), ((), ())), precision=lax.Precision.HIGHEST,
@@ -193,8 +216,25 @@
             total = total + buf[k]
         return total, copies
 
-    part, copies_y = reduce(gather_y, gram[...], gy, ny, red_send_y, red_recv_y, lambda t: (gx, t))
-    full, copies_x = reduce(gather_x, part, gx, nx, red_send_x, red_recv_x, lambda t: (t, gy))
+    lane_f = lax.broadcasted_iota(jnp.int32, (nf, LANES), 1)
+
+    def turn(v, by):
+        return pltpu.roll(v, by % LANES, 1) if by % LANES else v
+
+    packed = jnp.zeros((nf, LANES), jnp.float32)
+    for j in range(dep + 1):
+        kept = jnp.where(lane_f < (j + 1) * nf, gram[j * nf:(j + 1) * nf, :], 0.0)
+        packed = packed + turn(kept, nf * j * (j + 1) // 2)
+    part, copies_y = reduce(gather_y, packed, gy, ny, red_send_y, red_recv_y, lambda t: (gx, t))
+    whole, copies_x = reduce(gather_x, part, gx, nx, red_send_x, red_recv_x, lambda t: (t, gy))
+    wide[...] = jnp.zeros_like(wide)
+    for j in range(dep + 1):
+        wide[j * nf:(j + 1) * nf, :] = jnp.where(lane_f < (j + 1) * nf, turn(whole, -(nf * j * (j + 1) // 2)), 0.0)
+    lower = wide[...]
+    upper = jnp.transpose(lower)[0:nb]
+    lower = lower[0:nb]
+    block_row = lax.broadcasted_iota(jnp.int32, (nb, LANES), 0) // nf
+    full = jnp.where(lax.broadcasted_iota(jnp.int32, (nb, LANES), 1) < (block_row + 1) * nf, lower, upper)
 
     lane_b = lax.broadcasted_iota(jnp.int32, (nb, LANES), 1)
     sigma_lane = jnp.zeros((nb, LANES), jnp.float32)
@@ -246,11 +286,13 @@
             corr_ref[rows, :] = out[0:nf, span]
             new_ref[rows, :] = basis[0:nf, span] - out[nf:2 * nf, span]
 
-    wait_send(has_up, up_copies)
-    wait_send(has_down, down_copies)
-    for i in range(3):
-        wait_send(has_right, right_copies[i])
-        wait_send(has_left, left_copies[i])
+    for i in range(step):
+        swap[i].wait_send()
+        when(can_forward, lambda i=i: forward[i].wait_send())
+    for pairs, pred in ((own_edges, True), (near_edges, True), (far_edges, gets_forward)):
+        for pair in pairs:
+            when(has_right & pred, lambda pair=pair: pair[0].wait_send())
+            when(has_left & pred, lambda pair=pair: pair[1].wait_send())
     for c in copies_y + copies_x:
         c.wait_send()
 
@@ -271,6 +313,8 @@
         def untile(v):
             return v.reshape(nf, cx, nt, cy, LANES).transpose(0, 1, 3, 2, 4).reshape(nf, cx, cy, nz)
 
+        assert cx == DEPTH and nx % 2 == 0
+        halo_slots = 2 * (DEPTH + 1) + 4 + 4 * (DEPTH + 1)
         vmem = pl.BlockSpec(memory_space=pltpu.VMEM)
         corr, new, est = pl.pallas_call(
             functools.partial(kernel, nx, ny, (nf, cx, cy, nz)),
@@ -279,21 +323,21 @@
             out_specs=(vmem, vmem, vmem),
             scratch_shapes=[
                 pltpu.VMEM((DEPTH, wx, wy, nf, nz), jnp.float32),
-                pltpu.VMEM((wx, wy, nf, nz), jnp.float32),
+                pltpu.VMEM((DEPTH, wx, wy, nf, nz), jnp.float32),
                 pltpu.VMEM((wx, 3, cy, nz), jnp.float32),
                 pltpu.VMEM((nb, cx * cy * nz), jnp.float32),
                 pltpu.VMEM((nb, LANES), jnp.float32),
-                pltpu.VMEM((ny, nb, LANES), jnp.float32),
-                pltpu.VMEM((nx, nb, LANES), jnp.float32),
+                pltpu.VMEM((ny, nf, LANES), jnp.float32),
+                pltpu.VMEM((nx, nf, LANES), jnp.float32),
                 pltpu.VMEM((LANES, LANES), jnp.float32),
-                pltpu.SemaphoreType.DMA((16,)),
-                pltpu.SemaphoreType.DMA((16,)),
+                pltpu.SemaphoreType.DMA((halo_slots,)),
+                pltpu.SemaphoreType.DMA((halo_slots,)),
                 pltpu.SemaphoreType.DMA((ny,)),
                 pltpu.SemaphoreType.DMA((ny,)),
                 pltpu.SemaphoreType.DMA((nx,)),
                 pltpu.SemaphoreType.DMA((nx,)),
             ],
-            compiler_params=pltpu.CompilerParams(collective_id=0, has_side_effects=True),
+            compiler_params=pltpu.CompilerParams(collective_id=0, has_side_effects=True, vmem_limit_bytes=24 << 20),
         )(tiles(residual_block), diagonal)
         return untile(corr), untile(new), est[0, :nf]
 

time: 49.9 us -> 42.3 us (0.85)
  Pallas kernels: 45.5 us -> 37.9 us
    pallas_call x1, Pallas kernels: 45.5 us -> 37.9 us  [body(): pl.pallas_call(functools.partial(kernel, nx, ny, (nf, cx, cy, nz)), out_s...]
where the time goes in v2:
time: 42.3 us; the launch traced here: 42.1 us
  Pallas kernels  37.9 us (90%)
  local copies, waits for them, and re-layouts  3.62 us (9%)
  between operations  0.65 us (2%)
    pallas_call x1, Pallas kernels, body(): pl.pallas_call(functools.partial(kernel, nx, ny, (nf, cx, cy, nz)), out_s...  37.9 us
    unnamed x6, local copies, waits for them, and re-layouts  3.1 us

profile of v2, /device:TPU:0, one launch (start us, length us, event | category | flops | bytes accessed | tf_op | source)
XLA Modules:
  0.0 42.1 jit_solution(12137286706838402309)
XLA Ops:
  0.6 0.0 copy-start
  0.6 0.9 %copy-done = f32[8,4,8,256]{3,2,1,0:T(8,128)S(1)} copy-done((f32[8,4,8,256]{3,2,1,0:T(8,128)S(1)}, f32[8,4,8,256]{3,2,1,0:T(8,128)}, u32[]{:S(2)}) %copy-start) | copy-done | bytes 262168
  1.6 0.0 copy-start.1
  1.6 0.8 %copy-done.1 = f32[4,8,256]{2,1,0:T(8,128)S(1)} copy-done((f32[4,8,256]{2,1,0:T(8,128)S(1)}, f32[4,8,256]{2,1,0:T(8,128)}, u32[]{:S(2)}) %copy-start.1) | copy-done | bytes 32792
  2.3 37.9 %shard_map.49 = (f32[512,128]{1,0:T(8,128)S(1)}, f32[512,128]{1,0:T(8,128)S(1)}, f32[1,128]{1,0:T(1,128)S(1)}) custom-call(f32[512,128]{1,0:T(8,128)S(1)} %bitcast.17, f32[4,8,256]{2,1,0:T(8,128)S(1)} %copy-done.1), custom_call_target="tpu_custom_call" | custom-call | tf_op jit(solution)/shard_map/pallas_call | solution.py:319
  40.2 0.5 %slice_bitcast_fusion = f32[8]{0:T(128)} fusion(f32[1,128]{1,0:T(1,128)S(1)} %get-tuple-element.8), kind=kLoop, calls=%fused_computation | loop fusion | bytes 64 | tf_op jit(solution)/shard_map/squeeze | solution.py:342
  40.7 0.7 %copy.7 = f32[8,4,8,256]{3,2,1,0:T(8,128)} copy(f32[8,4,8,256]{3,2,1,0:T(8,128)S(1)} %bitcast.19) | data formatting | bytes 524288
  41.4 0.7 %copy.8 = f32[8,4,8,256]{3,2,1,0:T(8,128)} copy(f32[8,4,8,256]{3,2,1,0:T(8,128)S(1)} %bitcast.18) | data formatting | bytes 524288
Async XLA Ops:
  0.6 1.0 %copy-start = (f32[8,4,8,256]{3,2,1,0:T(8,128)S(1)}, f32[8,4,8,256]{3,2,1,0:T(8,128)}, u32[]{:S(2)}) copy-start(f32[8,4,8,256]{3,2,1,0:T(8,128)} %param.2) | copy-start | bytes 786436
  1.6 0.8 %copy-start.1 = (f32[4,8,256]{2,1,0:T(8,128)S(1)}, f32[4,8,256]{2,1,0:T(8,128)}, u32[]{:S(2)}) copy-start(f32[4,8,256]{2,1,0:T(8,128)} %d_ref.1) | copy-start | bytes 98308

commit v3 on v2

--- a/solution.py
+++ b/solution.py
@@ -19,8 +19,8 @@
 LANES = 128
 
 
-def kernel(nx, ny, dims, r_ref, d_ref, corr_ref, new_ref, est_ref,
-           e_bufs, sy, dd, basis, gram, gather_y, gather_x, wide, halo_send, halo_recv, red_send_y, red_recv_y,
+def kernel(nx, ny, dims, r_hbm, d_hbm, basis, small_ref, r_ref, d_ref, load_sem,
+           e_bufs, sy, dd, gram, gather_y, gather_x, wide, halo_send, halo_recv, red_send_y, red_recv_y,
            red_send_x, red_recv_x):
     nf, cx, cy, nz = dims
     dep = DEPTH
@@ -38,14 +38,9 @@
     for k in range(1, ny):
         pl.semaphore_signal(barrier, inc=1, device_id=(gx, lax.rem(gy + k, ny)), device_id_type=MESH)
 
-    for x in range(cx):
-        for y in range(cy):
-            v = jnp.concatenate([r_ref[pl.ds((x * nt + t) * cy + y, nf, stride=cx * cy * nt), :] for t in range(nt)], 1)
-            e0[dep + x, dep + y] = v
-            cell = x * cy + y
-            basis[0:nf, cell * nz:(cell + 1) * nz] = v
-        dd[dep + x, 1] = d_ref[x]
-
+    loads = [pltpu.make_async_copy(r_hbm, r_ref, load_sem.at[0]), pltpu.make_async_copy(d_hbm, d_ref, load_sem.at[1])]
+    for c in loads:
+        c.start()
     even = lax.rem(gx, 2) == 0
     partner = jnp.where(even, gx + 1, gx - 1)
     beyond = jnp.where(even, gx + 2, gx - 2)
@@ -72,6 +67,17 @@
 
     pl.when(gy == 0)(lambda: clear_cols(0, 0))
     pl.when(gy == ny - 1)(lambda: clear_cols(dep + cy, 2))
+
+    for c in loads:
+        c.wait()
+
+    for x in range(cx):
+        for y in range(cy):
+            v = jnp.concatenate([r_ref[pl.ds((x * nt + t) * cy + y, nf, stride=cx * cy * nt), :] for t in range(nt)], 1)
+            e0[dep + x, dep + y] = v
+            cell = x * cy + y
+            basis[0:nf, cell * nz:(cell + 1) * nz] = v
+        dd[dep + x, 1] = d_ref[x]
 
     pl.semaphore_wait(barrier, nx + ny - 2)
 
@@ -264,8 +270,6 @@
 
     diag0 = jnp.sum(jnp.where(lane_k[:nf] == row_k[:nf], full[:nf], 0.0), axis=0, keepdims=True)
     used = pltpu.roll(jnp.sum(jnp.where(in_right, right_side * coeffs, 0.0), axis=0, keepdims=True), LANES - nk, 1)
-    est_ref[...] = (diag0 - used) / jnp.where(lane_k[:1] < nf, diag0, 1.0)
-
     blocks = [coeffs[j * nf:(j + 1) * nf] for j in range(dep)]
     combined = [SHIFTS[0] * blocks[0]]
     for j in range(1, dep):
@@ -275,16 +279,8 @@
     for j in range(dep + 1):
         moved = pltpu.roll(combined[j], nf, 1)
         wide[j * nf:(j + 1) * nf, :] = moved + blocks[j] if j < dep else moved
-    weights = jnp.transpose(wide[...])[nk:nk + 2 * nf, 0:nb]
-    out = lax.dot_general(weights, basis[...], (((1,), (0,)), ((), ())), precision=lax.Precision.HIGHEST,
-                          preferred_element_type=jnp.float32)
-    for cell in range(cx * cy):
-        x, y = cell // cy, cell % cy
-        for t in range(nt):
-            span = slice(cell * nz + t * LANES, cell * nz + (t + 1) * LANES)
-            rows = pl.ds((x * nt + t) * cy + y, nf, stride=cx * cy * nt)
-            corr_ref[rows, :] = out[0:nf, span]
-            new_ref[rows, :] = basis[0:nf, span] - out[nf:2 * nf, span]
+    small_ref[0:2 * nf, :] = jnp.transpose(wide[...])[nk:nk + 2 * nf, :]
+    small_ref[2 * nf:, :] = jnp.broadcast_to((diag0 - used) / jnp.where(lane_k[:1] < nf, diag0, 1.0), (nf, LANES))
 
     for i in range(step):
         swap[i].wait_send()
@@ -297,6 +293,34 @@
         c.wait_send()
 
 
+def combine(dims, basis, small, corr_hbm, new_hbm, est_ref, corr, new, sems):
+    nf, cx, cy, nz = dims
+    nt = nz // LANES
+    nb = (DEPTH + 1) * nf
+    weights = small[0:2 * nf, 0:nb]
+    copies = []
+    for x in range(cx):
+        at = x * cy * nz
+        part = basis[:, at:at + cy * nz]
+        out = lax.dot_general(weights, part, (((1,), (0,)), ((), ())), precision=lax.Precision.HIGHEST,
+                              preferred_element_type=jnp.float32)
+        for y in range(cy):
+            for t in range(nt):
+                span = slice(y * nz + t * LANES, y * nz + (t + 1) * LANES)
+                rows = pl.ds(t * cy + y, nf, stride=nt * cy)
+                corr[x, rows, :] = out[0:nf, span]
+                new[x, rows, :] = part[0:nf, span] - out[nf:2 * nf, span]
+        for i, (src, dst) in enumerate(((corr, corr_hbm), (new, new_hbm))):
+            for f in range(nf):
+                c = pltpu.make_async_copy(src.at[x, pl.ds(f * nt * cy, nt * cy)],
+                                          dst.at[pl.ds((f * cx + x) * nt * cy, nt * cy)], sems.at[i, x, f])
+                c.start()
+                copies.append(c)
+    est_ref[...] = small[2 * nf:2 * nf + 1, 0:nf]
+    for c in copies:
+        c.wait()
+
+
 def solution(mesh):
     nx, ny = mesh.shape["gx"], mesh.shape["gy"]
 
@@ -316,16 +340,20 @@
         assert cx == DEPTH and nx % 2 == 0
         halo_slots = 2 * (DEPTH + 1) + 4 + 4 * (DEPTH + 1)
         vmem = pl.BlockSpec(memory_space=pltpu.VMEM)
-        corr, new, est = pl.pallas_call(
+        hbm = pl.BlockSpec(memory_space=pltpu.HBM)
+        basis, small = pl.pallas_call(
             functools.partial(kernel, nx, ny, (nf, cx, cy, nz)),
-            out_shape=(flat, flat, jax.ShapeDtypeStruct((1, LANES), jnp.float32)),
-            in_specs=[vmem, vmem],
-            out_specs=(vmem, vmem, vmem),
+            out_shape=(jax.ShapeDtypeStruct((nb, cx * cy * nz), jnp.float32),
+                       jax.ShapeDtypeStruct((3 * nf, LANES), jnp.float32)),
+            in_specs=[hbm, hbm],
+            out_specs=(vmem, vmem),
             scratch_shapes=[
+                pltpu.VMEM(flat.shape, jnp.float32),
+                pltpu.VMEM(diagonal.shape, jnp.float32),
+                pltpu.SemaphoreType.DMA((2,)),
                 pltpu.VMEM((DEPTH, wx, wy, nf, nz), jnp.float32),
                 pltpu.VMEM((DEPTH, wx, wy, nf, nz), jnp.float32),
                 pltpu.VMEM((wx, 3, cy, nz), jnp.float32),
-                pltpu.VMEM((nb, cx * cy * nz), jnp.float32),
                 pltpu.VMEM((nb, LANES), jnp.float32),
                 pltpu.VMEM((ny, nf, LANES), jnp.float32),
                 pltpu.VMEM((nx, nf, LANES), jnp.float32),
@@ -338,8 +366,21 @@
                 pltpu.SemaphoreType.DMA((nx,)),
             ],
             compiler_params=pltpu.CompilerParams(collective_id=0, has_side_effects=True, vmem_limit_bytes=24 << 20),
-        )(tiles(residual_block), diagonal)
-        return untile(corr), untile(new), est[0, :nf]
+        )(pltpu.with_memory_space_constraint(tiles(residual_block), pltpu.HBM),
+          pltpu.with_memory_space_constraint(diagonal, pltpu.HBM))
+        corr, new, est = pl.pallas_call(
+            functools.partial(combine, (nf, cx, cy, nz)),
+            out_shape=(flat, flat, jax.ShapeDtypeStruct((1, nf), jnp.float32)),
+            in_specs=[vmem, vmem],
+            out_specs=(hbm, hbm, vmem),
+            scratch_shapes=[
+                pltpu.VMEM((cx, nf * nt * cy, LANES), jnp.float32),
+                pltpu.VMEM((cx, nf * nt * cy, LANES), jnp.float32),
+                pltpu.SemaphoreType.DMA((2, cx, nf)),
+            ],
+            compiler_params=pltpu.CompilerParams(vmem_limit_bytes=8 << 20),
+        )(basis, small)
+        return untile(corr), untile(new), est.reshape(nf)
 
     return jax.shard_map(body, mesh=mesh, in_specs=(P(None, "gx", "gy", None), P("gx", "gy", None)),
                          out_specs=(P(None, "gx", "gy", None), P(None, "gx", "gy", None), P()), check_vma=False)

time: 42.3 us -> 39.2 us (0.927)
  local copies, waits for them, and re-layouts: 3.62 us -> 0 us
  Pallas kernels: 37.9 us -> 38.4 us
    unnamed x6 -> x0, local copies, waits for them, and re-layouts: 3.1 us -> none
    pallas_call x0 -> x1, Pallas kernels: none -> 2.48 us  [body(): pl.pallas_call(functools.partial(combine, (nf, cx, cy, nz)), out_shape=(f...]
    pallas_call x1, Pallas kernels: 37.9 us -> 35.9 us  [body(): pl.pallas_call(functools.partial(kernel, nx, ny, (nf, cx, cy, nz)), out_s...]
    squeeze x1 -> x0, local copies, waits for them, and re-layouts: 0.51 us -> none  [body(): return (untile(corr), untile(new), est[0, :nf])]
where the time goes in v3:
time: 39.2 us; the launch traced here: 39 us
  Pallas kernels  38.4 us (98%)
  between operations  0.64 us (2%)
    pallas_call x1, Pallas kernels, body(): pl.pallas_call(functools.partial(kernel, nx, ny, (nf, cx, cy, nz)), out_s...  35.9 us
    pallas_call x1, Pallas kernels, body(): pl.pallas_call(functools.partial(combine, (nf, cx, cy, nz)), out_shape=(f...  2.48 us

profile of v3, /device:TPU:0, one launch (start us, length us, event | category | flops | bytes accessed | tf_op | source)
XLA Modules:
  0.0 39.0 jit_solution(10016508439484777090)
XLA Ops:
  0.6 35.9 %shard_map.49 = (f32[40,8192]{1,0:T(8,128)S(1)}, f32[24,128]{1,0:T(8,128)S(1)}) custom-call(f32[512,128]{1,0:T(8,128)} %bitcast.16, f32[4,8,256]{2,1,0:T(8,128)} %d_hbm.1), custom_call_target="tpu_custom_call" | custom-call | tf_op jit(solution)/shard_map/pallas_call | solution.py:344
  36.6 2.5 %shard_map.50 = (f32[512,128]{1,0:T(8,128)}, f32[512,128]{1,0:T(8,128)}, f32[1,8]{1,0:T(1,128)}) custom-call(f32[40,8192]{1,0:T(8,128)S(1)} %get-tuple-element.8.basis, f32[24,128]{1,0:T(8,128)S(1)} %get-tuple-element.9.small), custom_call_target="tpu_custom_call" | custom-call | tf_op jit(solution)/shard_map/pallas_call | solution.py:371

commit v4 on v3

--- a/solution.py
+++ b/solution.py
@@ -21,7 +21,7 @@
 
 def kernel(nx, ny, dims, r_hbm, d_hbm, basis, small_ref, r_ref, d_ref, load_sem,
            e_bufs, sy, dd, gram, gather_y, gather_x, wide, halo_send, halo_recv, red_send_y, red_recv_y,
-           red_send_x, red_recv_x):
+           red_send_x, red_recv_x, known):
     nf, cx, cy, nz = dims
     dep = DEPTH
     nb = (dep + 1) * nf
@@ -32,18 +32,34 @@
     wx, wy = cx + 2 * dep, cy + 2 * dep
     nt = nz // LANES
 
+    even = lax.rem(gx, 2) == 0
+    partner = jnp.where(even, gx + 1, gx - 1)
+    beyond = jnp.where(even, gx + 2, gx - 2)
+    has_up, has_down = gx < nx - 2, gx >= 2
+    gx_peers = 1 + jnp.where(has_up, 1, 0) + jnp.where(has_down, 1, 0)
+
+    def greet(sem):
+        pl.semaphore_signal(sem, inc=1, device_id=(partner, gy), device_id_type=MESH)
+        pl.when(has_up)(lambda: pl.semaphore_signal(sem, inc=1, device_id=(gx + 2, gy), device_id_type=MESH))
+        pl.when(has_down)(lambda: pl.semaphore_signal(sem, inc=1, device_id=(gx - 2, gy), device_id_type=MESH))
+
     barrier = pltpu.get_barrier_semaphore()
-    for k in range(1, nx):
-        pl.semaphore_signal(barrier, inc=1, device_id=(lax.rem(gx + k, nx), gy), device_id_type=MESH)
+    greet(barrier)
     for k in range(1, ny):
         pl.semaphore_signal(barrier, inc=1, device_id=(gx, lax.rem(gy + k, ny)), device_id_type=MESH)
+    rounds = nx // 2 - 1
+    done = []
+
+    def next_round():
+        if len(done) < rounds:
+            pl.semaphore_wait(known.at[len(done)], gx_peers)
+            done.append(1)
+            if len(done) < rounds:
+                greet(known.at[len(done)])
 
     loads = [pltpu.make_async_copy(r_hbm, r_ref, load_sem.at[0]), pltpu.make_async_copy(d_hbm, d_ref, load_sem.at[1])]
     for c in loads:
         c.start()
-    even = lax.rem(gx, 2) == 0
-    partner = jnp.where(even, gx + 1, gx - 1)
-    beyond = jnp.where(even, gx + 2, gx - 2)
     can_forward = (beyond >= 0) & (beyond < nx)
     gets_forward = (gx > 0) & (gx < nx - 1)
     has_right, has_left = gy < ny - 1, gy > 0
@@ -79,66 +95,86 @@
             basis[0:nf, cell * nz:(cell + 1) * nz] = v
         dd[dep + x, 1] = d_ref[x]
 
-    pl.semaphore_wait(barrier, nx + ny - 2)
+    pl.semaphore_wait(barrier, gx_peers + ny - 1)
+    if rounds > 0:
+        greet(known.at[0])
 
     def copy(src, dst, slot, dev):
         return pltpu.make_async_remote_copy(src_ref=src, dst_ref=dst, send_sem=halo_send.at[slot],
                                             recv_sem=halo_recv.at[slot], device_id=dev, device_id_type=MESH)
 
-    own_y = pl.ds(dep, cy)
-    step = dep + 1
-    swap = [copy(dd.at[pl.ds(dep, cx), 1], dd.at[pl.ds(far, cx), 1], 0, (partner, gy))]
-    swap += [copy(e0.at[dep + i, own_y], e0.at[far + i, own_y], 1 + i, (partner, gy)) for i in range(cx)]
-    forward = [copy(dd.at[pl.ds(near, cx), 1], dd.at[pl.ds(far, cx), 1], step, (beyond, gy))]
-    forward += [copy(e0.at[near + i, own_y], e0.at[far + i, own_y], step + 1 + i, (beyond, gy)) for i in range(cx)]
-
-    def edges(rows, drows, slot, d_only=False):
-        right, left = (gx, gy + 1), (gx, gy - 1)
-        if d_only:
-            return (copy(dd.at[drows, 1], dd.at[drows, 0], slot, right),
-                    copy(dd.at[drows, 1], dd.at[drows, 2], slot + 1, left))
-        return (copy(e0.at[rows, pl.ds(cy, dep)], e0.at[rows, pl.ds(0, dep)], slot, right),
-                copy(e0.at[rows, pl.ds(dep, dep)], e0.at[rows, pl.ds(dep + cy, dep)], slot + 1, left))
-
-    base = 2 * step
-    own_edges = [edges(None, pl.ds(dep, cx), base, True), edges(pl.ds(dep, cx), None, base + 2)]
-    base += 4
-    near_edges = [edges(None, pl.ds(near, cx), base, True)]
-    near_edges += [edges(near + i, None, base + 2 + 2 * i) for i in range(cx)]
-    base += 2 * step
-    far_edges = [edges(None, pl.ds(far, cx), base, True)]
-    far_edges += [edges(far + i, None, base + 2 + 2 * i) for i in range(cx)]
+    pieces = [(i, h) for i in range(cx) for h in range(2)]
+    pieces.insert(2, None)
+    count = len(pieces)
+    left_half, right_half = pl.ds(dep, dep), pl.ds(cy, dep)
+
+    def block(src, dev, slot):
+        out = []
+        for k, piece in enumerate(pieces):
+            if piece is None:
+                out.append(copy(dd.at[pl.ds(src, cx), 1], dd.at[pl.ds(far, cx), 1], slot + k, dev))
+            else:
+                half = (left_half, right_half)[piece[1]]
+                out.append(copy(e0.at[src + piece[0], half], e0.at[far + piece[0], half], slot + k, dev))
+        return out
+
+    swap = block(dep, (partner, gy), 0)
+    forward = block(near, (beyond, gy), count)
+    right, left = (gx, gy + 1), (gx, gy - 1)
+
+    def d_edges(rows, slot):
+        return (copy(dd.at[rows, 1], dd.at[rows, 0], slot, right), copy(dd.at[rows, 1], dd.at[rows, 2], slot + 1, left))
+
+    def e_edges(rows, slot):
+        return (copy(e0.at[rows, right_half], e0.at[rows, pl.ds(0, dep)], slot, right),
+                copy(e0.at[rows, left_half], e0.at[rows, pl.ds(dep + cy, dep)], slot + 1, left))
+
+    def block_edges(src, slot):
+        out = []
+        for k, piece in enumerate(pieces):
+            if piece is None:
+                out.append(d_edges(pl.ds(src, cx), slot + 2 * k))
+            else:
+                pair = e_edges(src + piece[0], slot + 2 * k)
+                out.append((None, pair[1]) if piece[1] == 0 else (pair[0], None))
+        return out
+
+    base = 2 * count
+    own_edges = [d_edges(pl.ds(dep, cx), base), e_edges(pl.ds(dep, cx), base + 2)]
+    near_edges = block_edges(near, base + 4)
+    far_edges = block_edges(far, base + 4 + 2 * count)
 
     def when(pred, act):
         pl.when(pred)(act)
 
-    def start_edges(pair, pred=True):
-        when(has_right & pred, lambda: pair[0].start())
-        when(has_left & pred, lambda: pair[1].start())
+    def each(pred, pairs, act, other=False):
+        for side, has in ((0, has_left if other else has_right), (1, has_right if other else has_left)):
+            def go(side=side):
+                for pair in pairs:
+                    if pair[side] is not None:
+                        act(pair[side])
+            if any(pair[side] is not None for pair in pairs):
+                when(has & pred, go)
+
+    def start_edges(pairs, pred=True):
+        each(pred, pairs, lambda c: c.start())
 
     def wait_edges(pairs, pred=True):
-        def low():
-            for pair in pairs:
-                pair[0].wait_recv()
-
-        def high():
-            for pair in pairs:
-                pair[1].wait_recv()
-        when(has_left & pred, low)
-        when(has_right & pred, high)
+        each(pred, pairs, lambda c: c.wait_recv(), other=True)
 
     for c in swap:
         c.start()
-    for pair in own_edges:
-        start_edges(pair)
-    for i in range(step):
+    start_edges(own_edges)
+    for i in range(count):
         swap[i].wait_recv()
         when(can_forward, lambda i=i: forward[i].start())
-        start_edges(near_edges[i])
-
-    def take_far(i):
-        when(gets_forward, lambda: forward[i].wait_recv())
-        start_edges(far_edges[i], gets_forward)
+        start_edges(near_edges[i:i + 1])
+    next_round()
+
+    def take_far(lo, hi):
+        for i in range(lo, min(hi, count)):
+            when(gets_forward, lambda i=i: forward[i].wait_recv())
+            start_edges(far_edges[i:i + 1], gets_forward)
 
     lane = lax.broadcasted_iota(jnp.int32, (nf, nz), 1)
     first, last = lane == 0, lane == nz - 1
@@ -182,14 +218,17 @@
         if count > 0:
             lax.fori_loop(0, count, body, 0)
 
+    take_far(0, 5)
     wait_edges(own_edges)
     wait_edges(near_edges)
-    take_far(0)
+    take_far(5, 7)
     for j in range(dep):
         lo = jnp.where(even, dep + j, j)
         sweep(row_pass, j, lo, cx + dep - 2 * j)
         sweep(col_pass, j, lo + 1, cx + dep - 2 - 2 * j)
-        take_far(1 + j)
+        if j == 0:
+            take_far(7, count)
+            next_round()
     wait_edges(far_edges, gets_forward)
     for j in range(dep):
         sweep(row_pass, j, jnp.where(even, j, cx + dep - j), dep)
@@ -232,6 +271,8 @@
         kept = jnp.where(lane_f < (j + 1) * nf, gram[j * nf:(j + 1) * nf, :], 0.0)
         packed = packed + turn(kept, nf * j * (j + 1) // 2)
     part, copies_y = reduce(gather_y, packed, gy, ny, red_send_y, red_recv_y, lambda t: (gx, t))
+    for _ in range(rounds):
+        next_round()
     whole, copies_x = reduce(gather_x, part, gx, nx, red_send_x, red_recv_x, lambda t: (t, gy))
     wide[...] = jnp.zeros_like(wide)
     for j in range(dep + 1):
@@ -282,13 +323,16 @@
     small_ref[0:2 * nf, :] = jnp.transpose(wide[...])[nk:nk + 2 * nf, :]
     small_ref[2 * nf:, :] = jnp.broadcast_to((diag0 - used) / jnp.where(lane_k[:1] < nf, diag0, 1.0), (nf, LANES))
 
-    for i in range(step):
+    for i in range(count):
         swap[i].wait_send()
-        when(can_forward, lambda i=i: forward[i].wait_send())
+
+    @pl.when(can_forward)
+    def _():
+        for i in range(count):
+            forward[i].wait_send()
+
     for pairs, pred in ((own_edges, True), (near_edges, True), (far_edges, gets_forward)):
-        for pair in pairs:
-            when(has_right & pred, lambda pair=pair: pair[0].wait_send())
-            when(has_left & pred, lambda pair=pair: pair[1].wait_send())
+        each(pred, pairs, lambda c: c.wait_send())
     for c in copies_y + copies_x:
         c.wait_send()
 
@@ -337,8 +381,8 @@
         def untile(v):
             return v.reshape(nf, cx, nt, cy, LANES).transpose(0, 1, 3, 2, 4).reshape(nf, cx, cy, nz)
 
-        assert cx == DEPTH and nx % 2 == 0
-        halo_slots = 2 * (DEPTH + 1) + 4 + 4 * (DEPTH + 1)
+        assert cx == DEPTH and cy == 2 * DEPTH and nx % 2 == 0
+        halo_slots = 6 * (2 * cx + 1) + 4
         vmem = pl.BlockSpec(memory_space=pltpu.VMEM)
         hbm = pl.BlockSpec(memory_space=pltpu.HBM)
         basis, small = pl.pallas_call(
@@ -364,6 +408,7 @@
                 pltpu.SemaphoreType.DMA((ny,)),
                 pltpu.SemaphoreType.DMA((nx,)),
                 pltpu.SemaphoreType.DMA((nx,)),
+                pltpu.SemaphoreType.REGULAR((max(nx // 2 - 1, 1),)),
             ],
             compiler_params=pltpu.CompilerParams(collective_id=0, has_side_effects=True, vmem_limit_bytes=24 << 20),
         )(pltpu.with_memory_space_constraint(tiles(residual_block), pltpu.HBM),

time: 39.2 us -> 37.3 us (0.952)
  Pallas kernels: 38.4 us -> 36.6 us
    pallas_call x1, Pallas kernels: 35.9 us -> 34.1 us  [body(): pl.pallas_call(functools.partial(kernel, nx, ny, (nf, cx, cy, nz)), out_s...]
where the time goes in v4:
time: 37.3 us; the launch traced here: 37.2 us
  Pallas kernels  36.6 us (98%)
  between operations  0.64 us (2%)
    pallas_call x1, Pallas kernels, body(): pl.pallas_call(functools.partial(kernel, nx, ny, (nf, cx, cy, nz)), out_s...  34.1 us
    pallas_call x1, Pallas kernels, body(): pl.pallas_call(functools.partial(combine, (nf, cx, cy, nz)), out_shape=(f...  2.49 us

profile of v4, /device:TPU:0, one launch (start us, length us, event | category | flops | bytes accessed | tf_op | source)
XLA Modules:
  0.0 37.2 jit_solution(14519577156229005089)
XLA Ops:
  0.6 34.1 %shard_map.49 = (f32[40,8192]{1,0:T(8,128)S(1)}, f32[24,128]{1,0:T(8,128)S(1)}) custom-call(f32[512,128]{1,0:T(8,128)} %bitcast.16, f32[4,8,256]{2,1,0:T(8,128)} %d_hbm.1), custom_call_target="tpu_custom_call" | custom-call | tf_op jit(solution)/shard_map/pallas_call | solution.py:388
  34.7 2.5 %shard_map.50 = (f32[512,128]{1,0:T(8,128)}, f32[512,128]{1,0:T(8,128)}, f32[1,8]{1,0:T(1,128)}) custom-call(f32[40,8192]{1,0:T(8,128)S(1)} %get-tuple-element.8.basis, f32[24,128]{1,0:T(8,128)S(1)} %get-tuple-element.9.small), custom_call_target="tpu_custom_call" | custom-call | tf_op jit(solution)/shard_map/pallas_call | solution.py:416
